TPU v7x, 256 devices: a whole 4x4x8 slice. The times are simulated.
256 devices in a mesh: row: 16 (over x, y), col: 16 (over z, core).
Axes of the slice: x: 4, y: 4, z: 8, core: 2. Of those that a mesh axis runs over, the one named last changes fastest.
Arguments:
- wrapped: float32 [1, 16384, 16384], P(None, 'row', 'col'), may hold values from -2.8 to 2.8
- col_steps: int32 [1, 16, 16], P(None, 'row', 'col'), may hold values from -2 to 2, as said below
- row_steps: int32 [1, 16, 16], P(None, 'row', 'col'), may hold values from -2 to 2, as said below
Outputs:
- unwrapped: float32 [1, 16384, 16384], P(None, 'row', 'col')
Inputs may be any that keep to these rules, and one draw needn't show every extreme that they name: `col_steps`: nonzero whole numbers; the last tile column has no edge. `row_steps`: nonzero whole numbers; the last tile row has no edge.
All inputs are finite; a program needn't handle non-finite values.
Results may differ from a plain program's by a relative error of at most 0.0003.
Values sent between devices are 32-bit elements; how exact they have to be, the bound alone decides.
A program may use at most 64 MiB of HBM per device.

v0:
```python
import math
import jax
import jax.numpy as jnp
from jax import lax
from jax.sharding import PartitionSpec as P

ITERS = 2
TWO_PI = 2.0 * math.pi


def with_halo(x, sides, width):
    edges = {}
    for axis, dim in sides:
        peers, length = (lax.axis_size(axis), x.shape[dim])
        up = [(i, (i + 1) % peers) for i in range(peers - 1)]
        last = lax.slice_in_dim(x, length - width, length, axis=dim)
        leading = lax.slice_in_dim(x, 0, width, axis=dim)
        edges[dim] = (
            lax.ppermute(last, axis, up),
            lax.ppermute(leading, axis, [(b, a) for a, b in up]),
        )
    done = []
    for _, dim in sides:
        low, high = edges[dim]
        around = [(width, width) if d in done else (0, 0) for d in range(x.ndim)]
        x = jnp.concatenate([jnp.pad(low, around), x, jnp.pad(high, around)], axis=dim)
        done.append(dim)
    return x


def gather_turned(arrays, axis, dims):
    turned = [jnp.moveaxis(a, dim, 0) for a, dim in zip(arrays, dims)]
    both = jnp.concatenate([t.reshape(len(t), -1) for t in turned], axis=1)
    result, at, finished = (lax.all_gather(both, axis, axis=0, tiled=True), 0, [])
    for t, dim in zip(turned, dims):
        piece = result[:, at : at + t[0].size].reshape(-1, *t.shape[1:])
        finished.append(jnp.moveaxis(piece, 0, dim))
        at += t[0].size
    return tuple(finished)


def wrap_diff(change):
    return change - TWO_PI * jnp.floor(change / TWO_PI + 0.5)


def running_sum(values):
    frames, tile_rows, tile_width = values.shape
    block_len = math.gcd(tile_width, 128)
    blocks_in = tile_width // block_len
    pieces = values.reshape(frames, tile_rows, blocks_in, block_len)
    strict_upper = (
        lax.broadcasted_iota(jnp.int32, (block_len, block_len), 0)
        < lax.broadcasted_iota(jnp.int32, (block_len, block_len), 1)
    ).astype(jnp.float32)
    inside = jnp.einsum("frcm,mk->frck", pieces, strict_upper, precision=lax.Precision.HIGHEST)
    totals = jnp.sum(pieces, axis=3)
    before = jnp.cumsum(totals, axis=2) - totals
    return (inside + before[:, :, :, None]).reshape(frames, tile_rows, tile_width)


def integrate_line(line):
    steps = wrap_diff(line[:, 1:] - line[:, :-1])
    running = jnp.cumsum(steps, axis=1)
    return line[:, 0:1] + jnp.concatenate([jnp.zeros_like(line[:, 0:1]), running], axis=1)


def mean_jump(own_edge, crossing, beyond, weights):
    return jnp.sum(weights * (own_edge + crossing - beyond), axis=1) / jnp.sum(weights, axis=1)


def on_device(wrapped, col_steps, row_steps):
    frames, tile_rows, tile_cols = wrapped.shape
    padded = with_halo(wrapped, (("row", 1), ("col", 2)), 1)
    step_x = wrap_diff(padded[:, :, 1:] - padded[:, :, :-1])
    step_y = wrap_diff(padded[:, 1:, :] - padded[:, :-1, :])
    charge_across = (
        step_x[:, 0:tile_rows, tile_cols - 1]
        + step_y[:, 0:tile_rows, tile_cols]
        - step_x[:, 1 : tile_rows + 1, tile_cols - 1]
        - step_y[:, 0:tile_rows, tile_cols - 1]
    ) / TWO_PI
    at_top = (lax.broadcasted_iota(jnp.int32, (1, tile_rows), 1) == 0) & (
        lax.axis_index("row") == 0
    )
    charge_across = jnp.where(at_top, 0.0, charge_across)
    charge_down = (
        step_x[:, tile_rows - 1, 0:tile_cols]
        + step_y[:, tile_rows - 1, 1 : tile_cols + 1]
        - step_x[:, tile_rows, 0:tile_cols]
        - step_y[:, tile_rows - 1, 0:tile_cols]
    ) / TWO_PI
    at_left = (lax.broadcasted_iota(jnp.int32, (1, tile_cols), 1) == 0) & (
        lax.axis_index("col") == 0
    )
    charge_down = jnp.where(at_left, 0.0, charge_down)
    weight_across = 1.0 / (1.0 + jnp.abs(charge_across))
    weight_down = 1.0 / (1.0 + jnp.abs(charge_down))
    crossing_x = step_x[:, 1 : tile_rows + 1, tile_cols]
    crossing_y = step_y[:, tile_rows, 1 : tile_cols + 1]
    column_steps = step_y[:, 1 : tile_rows + 1, 1]
    downward = jnp.cumsum(column_steps, axis=1) - column_steps
    anchor = wrapped[:, 0, 0]
    integrated = (anchor[:, None] + downward)[:, :, None] + running_sum(
        step_x[:, 1 : tile_rows + 1, 1 : tile_cols + 1]
    )
    cycles_across = TWO_PI * col_steps[:, 0, 0].astype(jnp.float32)
    cycles_down = TWO_PI * row_steps[:, 0, 0].astype(jnp.float32)
    right_first = integrate_line(padded[:, 1 : tile_rows + 1, tile_cols + 1])
    below_first = integrate_line(padded[:, tile_rows + 1, 1 : tile_cols + 1])
    base_across = (
        mean_jump(integrated[:, :, -1], crossing_x, right_first, weight_across) + cycles_across
    )
    base_down = mean_jump(integrated[:, -1, :], crossing_y, below_first, weight_down) + cycles_down
    grid_rows = lax.axis_size("row")
    grid_cols = lax.axis_size("col")
    every_across, every_down = gather_turned(
        (base_across[:, None], base_down[:, None]), ("row", "col"), (1, 1)
    )
    every_across = every_across.reshape(frames, grid_rows, grid_cols)
    every_down = every_down.reshape(frames, grid_rows, grid_cols)
    totals = jnp.zeros((frames, grid_rows, grid_cols), jnp.float32)
    for sweep in range(ITERS):
        right_total = jnp.concatenate(
            [totals[:, :, 1:], jnp.zeros((frames, grid_rows, 1), jnp.float32)], axis=2
        )
        below_total = jnp.concatenate(
            [totals[:, 1:, :], jnp.zeros((frames, 1, grid_cols), jnp.float32)], axis=1
        )
        horizontal = every_across + totals - right_total
        vertical = every_down + totals - below_total
        prefix_across = jnp.cumsum(horizontal, axis=2) - horizontal
        prefix_down = jnp.cumsum(vertical, axis=1) - vertical
        totals = totals + 0.5 * (
            prefix_across + prefix_across[:, 0:1, :] + prefix_down + prefix_down[:, :, 0:1]
        )
    mine = lax.dynamic_slice(
        totals, (0, lax.axis_index("row"), lax.axis_index("col")), (frames, 1, 1)
    )
    return (integrated + mine) / TWO_PI


def solution(mesh):
    in_specs = (P(None, "row", "col"), P(None, "row", "col"), P(None, "row", "col"))
    out_specs = P(None, "row", "col")
    return jax.shard_map(
        on_device, mesh=mesh, in_specs=in_specs, out_specs=out_specs, check_vma=False
    )
```

profile of v0, /device:TPU:1, one launch (start us, length us, event | category | flops | bytes accessed | tf_op | source)
XLA Modules:
  0.0 165.0 jit_solution(7441537384304579443)
XLA Ops:
  0.0 0.8 fusion.18
  1.0 4.1 %collective-permute-start.1 = (f32[1,1,1024]{1,2,0:T(8,128)S(1)}, f32[1,1,1024]{1,2,0:T(8,128)S(1)}, u32[]{:S(2)}, u32[]{:S(2)}) collective-permute-start(f32[1,1,1024]{1,2,0:T(8,128)S(1)} %copy.21), channel_id=1, source_target_pairs={{0,16},{16,32},{32,48},{48,64},{64,80},{80,96},{96,112},{112,128},... | collective-permute-start | bytes 12296 | tf_op jit(solution)/shard_map/ppermute | solution.py:19
  5.3 1.3 collective-permute-start.2
  6.6 5.3 %copy.20 = f32[1,1024,1024]{1,2,0:T(8,128)} copy(f32[1,1024,1024]{2,1,0:T(8,128)} %param.3) | data formatting | bytes 8388608 | tf_op args[0]
  11.9 0.8 fusion.17
  12.7 2.9 %collective-permute-start.3 = (f32[1,1024,1]{1,2,0:T(1,128)S(1)}, f32[1,1024,1]{1,2,0:T(1,128)S(1)}, u32[]{:S(2)}, u32[]{:S(2)}) collective-permute-start(f32[1,1024,1]{1,2,0:T(1,128)S(1)} %get-tuple-element.13), channel_id=1, source_target_pairs={{1,0},{2,1},{3,2},{4,3},{5,4},{6,5},{7,6},{8,7},{9,8},{10,9},{11,1... | collective-permute-start | bytes 12296 | tf_op jit(solution)/shard_map/ppermute | solution.py:20
  15.6 3.4 %collective-permute-start = (f32[1,1024,1]{1,2,0:T(1,128)S(1)}, f32[1,1024,1]{1,2,0:T(1,128)S(1)}, u32[]{:S(2)}, u32[]{:S(2)}) collective-permute-start(f32[1,1024,1]{1,2,0:T(1,128)S(1)} %get-tuple-element.14), channel_id=1, source_target_pairs={{0,1},{1,2},{2,3},{3,4},{4,5},{5,6},{6,7},{7,8},{8,9},{9,10},{10,1... | collective-permute-start | bytes 12296 | tf_op jit(solution)/shard_map/ppermute | solution.py:19
  19.1 1.3 slice.130
  22.0 0.6 slice.192
  22.6 0.5 slice.183
  23.2 6.4 %concatenate.59 = f32[1,1026,1024]{1,2,0:T(8,128)} concatenate(f32[1,1,1024]{1,2,0:T(8,128)S(1)} %collective-permute-done.1, f32[1,1024,1024]{1,2,0:T(8,128)} %copy.20, f32[1,1,1024]{1,2,0:T(8,128)S(1)} %collective-permute-done.2), dimensions={1} | concatenate | bytes 8404992 | tf_op jit(solution)/shard_map/concatenate | solution.py:26
  29.7 7.4 %multiply_subtract_fusion = f32[1,1026,1025]{1,2,0:T(8,128)} fusion(f32[1,1026,1024]{1,2,0:T(8,128)} %concatenate.59, f32[1,1026,1]{1,2,0:T(1,128)S(1)} %pad.15, f32[1,1026,1]{1,2,0:T(1,128)S(1)} %pad.16), kind=kLoop, calls=%fused_computation.2 | loop fusion | flops 8413200 | bytes 8417304 | tf_op jit(solution)/shard_map/sub | solution.py:43
  37.0 15.3 %concatenate.60 = f32[1,1026,1026]{1,2,0:T(8,128)} concatenate(f32[1,1026,1]{1,2,0:T(1,128)S(1)} %pad.15, f32[1,1026,1024]{1,2,0:T(8,128)} %concatenate.59, f32[1,1026,1]{1,2,0:T(1,128)S(1)} %pad.16), dimensions={2} | concatenate | bytes 8421408 | tf_op jit(solution)/shard_map/concatenate | solution.py:26
  52.3 0.3 reduce-window.26
  53.0 0.3 reduce-window.24
  53.6 5.1 %multiply_subtract_fusion.1 = f32[1,1025,1026]{1,2,0:T(8,128)S(1)} fusion(f32[1,1026,1026]{1,2,0:T(8,128)} %concatenate.60), kind=kLoop, calls=%fused_computation.3 | loop fusion | flops 6309900 | bytes 12619800 | tf_op jit(solution)/shard_map/sub | solution.py:43
  58.8 2.2 %copy-done.1 = f32[1,1025,1026]{1,2,0:T(8,128)} copy-done((f32[1,1025,1026]{1,2,0:T(8,128)}, f32[1,1025,1026]{1,2,0:T(8,128)S(1)}, u32[]{:S(2)}) %copy-start.1) | copy-done | bytes 4206624
  61.7 5.7 %slice.176 = f32[1,1024,1024]{1,2,0:T(8,128)} slice(f32[1,1026,1025]{1,2,0:T(8,128)} %multiply_subtract_fusion), slice={[0:1], [1:1025], [1:1025]} | slice | bytes 8388608 | tf_op jit(solution)/shard_map/slice | solution.py:104
  67.4 2.6 %reduce_sum.45 = f32[1024,8]{0,1:T(8,128)S(1)} reduce(f32[1024,8,128]{0,2,1:T(8,128)} %bitcast.62, f32[]{:T(128)} %constant.51.clone.1), dimensions={2}, to_apply=%region_2.3 | reduce | flops 1040384 | bytes 4227076 | tf_op jit(solution)/shard_map/reduce_sum | solution.py:56
  70.1 5.3 %convolution_add_fusion = f32[1024,8,128]{0,2,1:T(8,128)S(1)} fusion(f32[1024,8,128]{0,2,1:T(8,128)} %bitcast.63, f32[1024,8]{0,1:T(8,128)S(1)} %sub.200), kind=kOutput, calls=%fused_computation.6 | convolution fusion | flops 1611677696 | bytes 8421376 | tf_op jit(solution)/shard_map/frcm,mk->frck/dot_general | solution.py:55
  75.4 1.5 subtract_add_fusion
  77.0 0.8 bitcast_add_fusion
  77.8 2.6 %fusion = (f32[1024]{0:T(1024)S(1)}, f32[1024]{0:T(1024)S(1)}) fusion(f32[1,1025,1026]{1,2,0:T(8,128)} %copy-done.1, f32[1,1024,1024]{1,2,0:T(8,128)S(1)} %bitcast_add_fusion, f32[1,1026,1025]{1,2,0:T(8,128)} %multiply_subtract_fusion), kind=kLoop, calls=%fused_computation.8 | loop fusion | flops 5120 | bytes 32768 | tf_op jit(solution)/shard_map/add | solution.py:68
  80.6 2.9 %fusion.15 = (f32[]{:T(128)}, f32[]{:T(128)}, f32[]{:T(128)}, f32[]{:T(128)}) fusion(f32[1,1023]{1,0:T(1,128)S(1)} %slice_add_fusion.3, f32[1,1]{1,0:T(1,128)} %constant.59.clone.1, f32[]{:T(128)} %bitcast.12, f32[1,1026,1025]{1,2,0:T(8,128)} %multiply_subtract_fusion, f32[1,1024,1024]{1,2,0:T(8,128)S(1)} %bitcast_add_fusion, f32[1,1025,1026]{1,2,0:T(8,128)} %copy-done.1, ...), kind=kLoop, calls=%fused_computation.62 | loop fusion | flops 28668 | bytes 40982 | tf_op jit(solution)/shard_map/reduce_sum | solution.py:68
  86.2 60.9 %all-gather = f32[256,1,2]{2,1,0:T(1,128)S(1)} all-gather(f32[1,1,2]{2,1,0:T(1,128)S(1)} %maximum_bitcast_fusion), channel_id=1, replica_groups=mesh['row'=16,'col'=16] {'row','col'}, dimensions={0}, use_global_device_ids=true | all-gather | bytes 2056 | tf_op jit(solution)/shard_map/all_gather | solution.py:34
  148.4 0.7 dynamic-slice.1
  149.1 0.6 dynamic-slice
  149.6 1.2 fusion.19
  150.8 1.2 fusion.20
  153.4 0.6 fusion.21
  154.0 5.7 %add_multiply_fusion = f32[1,1024,1024]{1,2,0:T(8,128)} fusion(f32[]{:T(128)} %bitcast.32, f32[1024,8,128]{0,2,1:T(8,128)} %copy-done, f32[1024]{0:T(1024)S(1)} %bitcast.66), kind=kLoop, calls=%fused_computation.5 | loop fusion | flops 3145728 | bytes 8392708 | tf_op jit(solution)/shard_map/div | solution.py:139
  159.7 5.3 %copy.26 = f32[1,1024,1024]{2,1,0:T(8,128)} copy(f32[1,1024,1024]{1,2,0:T(8,128)} %add_multiply_fusion) | data formatting | bytes 8388608 | tf_op jit(solution)/shard_map/div | solution.py:139
  (54 shorter events, 4.0 us)
Async XLA Ops:
  1.0 22.1 %collective-permute-start.1 = (f32[1,1,1024]{1,2,0:T(8,128)S(1)}, f32[1,1,1024]{1,2,0:T(8,128)S(1)}, u32[]{:S(2)}, u32[]{:S(2)}) collective-permute-start(f32[1,1,1024]{1,2,0:T(8,128)S(1)} %copy.21), channel_id=1, source_target_pairs={{0,16},{16,32},{32,48},{48,64},{64,80},{80,96},{96,112},{112,128},... | collective-permute-start | bytes 12296 | tf_op jit(solution)/shard_map/ppermute | solution.py:19
  5.3 16.3 %collective-permute-start.2 = (f32[1,1,1024]{1,2,0:T(8,128)S(1)}, f32[1,1,1024]{1,2,0:T(8,128)S(1)}, u32[]{:S(2)}, u32[]{:S(2)}) collective-permute-start(f32[1,1,1024]{1,2,0:T(8,128)S(1)} %copy.22), channel_id=1, source_target_pairs={{16,0},{32,16},{48,32},{64,48},{80,64},{96,80},{112,96},{128,112},... | collective-permute-start | bytes 12296 | tf_op jit(solution)/shard_map/ppermute | solution.py:20
  12.7 9.2 %collective-permute-start.3 = (f32[1,1024,1]{1,2,0:T(1,128)S(1)}, f32[1,1024,1]{1,2,0:T(1,128)S(1)}, u32[]{:S(2)}, u32[]{:S(2)}) collective-permute-start(f32[1,1024,1]{1,2,0:T(1,128)S(1)} %get-tuple-element.13), channel_id=1, source_target_pairs={{1,0},{2,1},{3,2},{4,3},{5,4},{6,5},{7,6},{8,7},{9,8},{10,9},{11,1... | collective-permute-start | bytes 12296 | tf_op jit(solution)/shard_map/ppermute | solution.py:20
  15.6 14.0 %collective-permute-start = (f32[1,1024,1]{1,2,0:T(1,128)S(1)}, f32[1,1024,1]{1,2,0:T(1,128)S(1)}, u32[]{:S(2)}, u32[]{:S(2)}) collective-permute-start(f32[1,1024,1]{1,2,0:T(1,128)S(1)} %get-tuple-element.14), channel_id=1, source_target_pairs={{0,1},{1,2},{2,3},{3,4},{4,5},{5,6},{6,7},{7,8},{8,9},{9,10},{10,1... | collective-permute-start | bytes 12296 | tf_op jit(solution)/shard_map/ppermute | solution.py:19
  58.7 2.2 %copy-start.1 = (f32[1,1025,1026]{1,2,0:T(8,128)}, f32[1,1025,1026]{1,2,0:T(8,128)S(1)}, u32[]{:S(2)}) copy-start(f32[1,1025,1026]{1,2,0:T(8,128)S(1)} %multiply_subtract_fusion.1) | copy-start | bytes 12619804
  75.4 5.1 %copy-start = (f32[1024,8,128]{0,2,1:T(8,128)}, f32[1024,8,128]{0,2,1:T(8,128)S(1)}, u32[]{:S(2)}) copy-start(f32[1024,8,128]{0,2,1:T(8,128)S(1)} %convolution_add_fusion) | copy-start | bytes 12582916
where the time goes:
time: 166 us; the launch traced here: 165 us
  blocking collectives  60.9 us (37%)
  local copies, waits for them, and re-layouts  47.6 us (29%)
  other arithmetic  34.1 us (21%)
  starting transfers between devices  11.6 us (7%)
  between operations  5.5 us (3%)
  matrix products  5.29 us (3%)
    all_gather x1, blocking collectives, gather_turned(): lax.all_gather(both, axis, axis=0, tiled=True)  60.9 us
    concatenate x2, local copies, waits for them, and re-layouts, with_halo(): jnp.concatenate([jnp.pad(low, around), x, jnp.pad(high, around)], axis=dim)  21.6 us
    sub x4, other arithmetic, wrap_diff(): return change - TWO_PI * jnp.floor(change / TWO_PI + 0.5)  12.6 us
    unnamed x5, local copies, waits for them, and re-layouts  7.52 us
    ppermute x2, starting transfers between devices, with_halo(): lax.ppermute(last, axis, up)  7.49 us
    slice x1, local copies, waits for them, and re-layouts, on_device(): step_x[:, 1:tile_rows + 1, 1:tile_cols + 1]  5.75 us
    div x1, other arithmetic, on_device(): return (integrated + mine) / TWO_PI  5.7 us
    div x1, local copies, waits for them, and re-layouts, on_device(): return (integrated + mine) / TWO_PI  5.34 us
  transfers between devices with their start and end apart: 4, of which 0 were waited for; matrix products, arithmetic and copies ran while one was open for 9% of the time, Pallas kernels for 0%

commit v1 on v0

--- a/solution.py
+++ b/solution.py
@@ -6,6 +6,11 @@
 
 ITERS = 2
 TWO_PI = 2.0 * math.pi
+
+
+def all_by_exchange(block, name, d):
+    stack = jnp.stack([block] * lax.axis_size(name))
+    return jnp.concatenate(lax.all_to_all(stack, name, 0, 0), axis=d)
 
 
 def with_halo(x, sides, width):
@@ -31,7 +36,7 @@
 def gather_turned(arrays, axis, dims):
     turned = [jnp.moveaxis(a, dim, 0) for a, dim in zip(arrays, dims)]
     both = jnp.concatenate([t.reshape(len(t), -1) for t in turned], axis=1)
-    result, at, finished = (lax.all_gather(both, axis, axis=0, tiled=True), 0, [])
+    result, at, finished = (all_by_exchange(both, axis, 0), 0, [])
     for t, dim in zip(turned, dims):
         piece = result[:, at : at + t[0].size].reshape(-1, *t.shape[1:])
         finished.append(jnp.moveaxis(piece, 0, dim))

time: 166 us -> 134 us (0.81)
  blocking collectives: 60.9 us -> 0 us
  starting transfers between devices: 11.6 us -> 26.9 us
  waiting for transfers between devices: 0.01 us -> 12.9 us
    all_gather x1 -> x0, blocking collectives: 60.9 us -> none  [gather_turned(): lax.all_gather(both, axis, axis=0, tiled=True)]
    all_to_all x0 -> x1, starting transfers between devices: none -> 15.2 us  [all_by_exchange(): return jnp.concatenate(lax.all_to_all(stack, name, 0, 0), axis=d)]
    all_to_all x0 -> x1, waiting for transfers between devices: none -> 12.9 us  [all_by_exchange(): return jnp.concatenate(lax.all_to_all(stack, name, 0, 0), axis=d)]
  transfers between devices with their start and end apart: 4 -> 5, of which waited for: 0 -> 1; matrix products, arithmetic and copies ran while one was open for 9% -> 12% of each run, Pallas kernels for 0% -> 0%
where the time goes in v1:
time: 134 us; the launch traced here: 133 us
  local copies, waits for them, and re-layouts  48.3 us (36%)
  other arithmetic  34.1 us (25%)
  starting transfers between devices  26.9 us (20%)
  waiting for transfers between devices  12.9 us (10%)
  between operations  5.5 us (4%)
  matrix products  5.29 us (4%)
    concatenate x2, local copies, waits for them, and re-layouts, with_halo(): jnp.concatenate([jnp.pad(low, around), x, jnp.pad(high, around)], axis=dim)  21.6 us
    all_to_all x1, starting transfers between devices, all_by_exchange(): return jnp.concatenate(lax.all_to_all(stack, name, 0, 0), axis=d)  15.2 us
    all_to_all x1, waiting for transfers between devices, all_by_exchange(): return jnp.concatenate(lax.all_to_all(stack, name, 0, 0), axis=d)  12.9 us
    sub x4, other arithmetic, wrap_diff(): return change - TWO_PI * jnp.floor(change / TWO_PI + 0.5)  12.6 us
    unnamed x5, local copies, waits for them, and re-layouts  7.52 us
    ppermute x2, starting transfers between devices, with_halo(): lax.ppermute(last, axis, up)  7.49 us
    slice x1, local copies, waits for them, and re-layouts, on_device(): step_x[:, 1:tile_rows + 1, 1:tile_cols + 1]  5.75 us
    div x1, other arithmetic, on_device(): return (integrated + mine) / TWO_PI  5.7 us
  transfers between devices with their start and end apart: 5, of which 1 were waited for; matrix products, arithmetic and copies ran while one was open for 12% of the time, Pallas kernels for 0%

profile of v1, /device:TPU:1, one launch (start us, length us, event | category | flops | bytes accessed | tf_op | source)
XLA Modules:
  0.0 133.0 jit_solution(1934995955906061356)
XLA Ops:
  0.0 0.8 fusion.18
  1.0 4.1 %collective-permute-start.1 = (f32[1,1,1024]{1,2,0:T(8,128)S(1)}, f32[1,1,1024]{1,2,0:T(8,128)S(1)}, u32[]{:S(2)}, u32[]{:S(2)}) collective-permute-start(f32[1,1,1024]{1,2,0:T(8,128)S(1)} %copy.28), channel_id=1, source_target_pairs={{0,16},{16,32},{32,48},{48,64},{64,80},{80,96},{96,112},{112,128},... | collective-permute-start | bytes 12296 | tf_op jit(solution)/shard_map/ppermute | solution.py:24
  5.3 1.3 collective-permute-start.2
  6.6 5.3 %copy.27 = f32[1,1024,1024]{1,2,0:T(8,128)} copy(f32[1,1024,1024]{2,1,0:T(8,128)} %param.3) | data formatting | bytes 8388608 | tf_op args[0]
  11.9 0.8 fusion.17
  12.7 2.9 %collective-permute-start.3 = (f32[1,1024,1]{1,2,0:T(1,128)S(1)}, f32[1,1024,1]{1,2,0:T(1,128)S(1)}, u32[]{:S(2)}, u32[]{:S(2)}) collective-permute-start(f32[1,1024,1]{1,2,0:T(1,128)S(1)} %get-tuple-element.13), channel_id=1, source_target_pairs={{1,0},{2,1},{3,2},{4,3},{5,4},{6,5},{7,6},{8,7},{9,8},{10,9},{11,1... | collective-permute-start | bytes 12296 | tf_op jit(solution)/shard_map/ppermute | solution.py:25
  15.6 3.4 %collective-permute-start = (f32[1,1024,1]{1,2,0:T(1,128)S(1)}, f32[1,1024,1]{1,2,0:T(1,128)S(1)}, u32[]{:S(2)}, u32[]{:S(2)}) collective-permute-start(f32[1,1024,1]{1,2,0:T(1,128)S(1)} %get-tuple-element.14), channel_id=1, source_target_pairs={{0,1},{1,2},{2,3},{3,4},{4,5},{5,6},{6,7},{7,8},{8,9},{9,10},{10,1... | collective-permute-start | bytes 12296 | tf_op jit(solution)/shard_map/ppermute | solution.py:24
  19.0 1.3 slice.130
  22.0 0.6 slice.192
  22.6 0.5 slice.183
  23.1 6.4 %concatenate.61 = f32[1,1026,1024]{1,2,0:T(8,128)} concatenate(f32[1,1,1024]{1,2,0:T(8,128)S(1)} %collective-permute-done.1, f32[1,1024,1024]{1,2,0:T(8,128)} %copy.27, f32[1,1,1024]{1,2,0:T(8,128)S(1)} %collective-permute-done.2), dimensions={1} | concatenate | bytes 8404992 | tf_op jit(solution)/shard_map/concatenate | solution.py:31
  29.7 7.4 %multiply_subtract_fusion = f32[1,1026,1025]{1,2,0:T(8,128)} fusion(f32[1,1026,1024]{1,2,0:T(8,128)} %concatenate.61, f32[1,1026,1]{1,2,0:T(1,128)S(1)} %pad.15, f32[1,1026,1]{1,2,0:T(1,128)S(1)} %pad.16), kind=kLoop, calls=%fused_computation.2 | loop fusion | flops 8413200 | bytes 8417304 | tf_op jit(solution)/shard_map/sub | solution.py:48
  37.0 15.3 %concatenate.62 = f32[1,1026,1026]{1,2,0:T(8,128)} concatenate(f32[1,1026,1]{1,2,0:T(1,128)S(1)} %pad.15, f32[1,1026,1024]{1,2,0:T(8,128)} %concatenate.61, f32[1,1026,1]{1,2,0:T(1,128)S(1)} %pad.16), dimensions={2} | concatenate | bytes 8421408 | tf_op jit(solution)/shard_map/concatenate | solution.py:31
  53.6 5.1 %multiply_subtract_fusion.1 = f32[1,1025,1026]{1,2,0:T(8,128)S(1)} fusion(f32[1,1026,1026]{1,2,0:T(8,128)} %concatenate.62), kind=kLoop, calls=%fused_computation.3 | loop fusion | flops 6309900 | bytes 12619800 | tf_op jit(solution)/shard_map/sub | solution.py:48
  58.7 2.2 %copy-done.1 = f32[1,1025,1026]{1,2,0:T(8,128)} copy-done((f32[1,1025,1026]{1,2,0:T(8,128)}, f32[1,1025,1026]{1,2,0:T(8,128)S(1)}, u32[]{:S(2)}) %copy-start.1) | copy-done | bytes 4206624
  61.6 5.7 %slice.176 = f32[1,1024,1024]{1,2,0:T(8,128)} slice(f32[1,1026,1025]{1,2,0:T(8,128)} %multiply_subtract_fusion), slice={[0:1], [1:1025], [1:1025]} | slice | bytes 8388608 | tf_op jit(solution)/shard_map/slice | solution.py:109
  67.4 2.6 %reduce_sum.45 = f32[1024,8]{0,1:T(8,128)S(1)} reduce(f32[1024,8,128]{0,2,1:T(8,128)} %bitcast.62, f32[]{:T(128)} %constant.51.clone.1), dimensions={2}, to_apply=%region_2.3 | reduce | flops 1040384 | bytes 4227076 | tf_op jit(solution)/shard_map/reduce_sum | solution.py:61
  70.1 5.3 %convolution_add_fusion = f32[1024,8,128]{0,2,1:T(8,128)S(1)} fusion(f32[1024,8,128]{0,2,1:T(8,128)} %bitcast.63, f32[1024,8]{0,1:T(8,128)S(1)} %sub.200), kind=kOutput, calls=%fused_computation.6 | convolution fusion | flops 1611677696 | bytes 8421376 | tf_op jit(solution)/shard_map/frcm,mk->frck/dot_general | solution.py:60
  75.4 1.5 %subtract_add_fusion = f32[1,1024,1]{1,2,0:T(1,128)S(1)} fusion(f32[1,1024,1]{1,2,0:T(1,128)S(1)} %bitcast.73, f32[1,1024,1]{1,2,0:T(1,128)S(1)} %bitcast.81, f32[]{:T(128)} %bitcast, f32[1,1025,1026]{1,2,0:T(8,128)} %copy-done.1), kind=kLoop, calls=%fused_computation.49 | loop fusion | flops 3072 | bytes 16388 | tf_op jit(solution)/shard_map/add | solution.py:108
  77.0 0.8 bitcast_add_fusion
  77.8 2.6 %fusion = (f32[1024]{0:T(1024)S(1)}, f32[1024]{0:T(1024)S(1)}) fusion(f32[1,1025,1026]{1,2,0:T(8,128)} %copy-done.1, f32[1,1024,1024]{1,2,0:T(8,128)S(1)} %bitcast_add_fusion, f32[1,1026,1025]{1,2,0:T(8,128)} %multiply_subtract_fusion), kind=kLoop, calls=%fused_computation.8 | loop fusion | flops 5120 | bytes 32768 | tf_op jit(solution)/shard_map/add | solution.py:73
  80.6 2.9 %fusion.15 = (f32[]{:T(128)}, f32[]{:T(128)}, f32[]{:T(128)}, f32[]{:T(128)}) fusion(f32[1,1023]{1,0:T(1,128)S(1)} %slice_add_fusion.3, f32[1,1]{1,0:T(1,128)} %constant.59.clone.1, f32[]{:T(128)} %bitcast.12, f32[1,1026,1025]{1,2,0:T(8,128)} %multiply_subtract_fusion, f32[1,1024,1024]{1,2,0:T(8,128)S(1)} %bitcast_add_fusion, f32[1,1025,1026]{1,2,0:T(8,128)} %copy-done.1, ...), kind=kLoop, calls=%fused_computation.62 | loop fusion | flops 28668 | bytes 40982 | tf_op jit(solution)/shard_map/reduce_sum | solution.py:73
  86.2 0.7 stack.2
  86.9 15.2 %all-to-all-start = ((f32[256,1,2]{2,1,0:T(1,128)}), f32[256,1,2]{2,1,0:T(1,128)S(1)}, u32[]{:S(2)}, u32[]{:S(2)}) async-start(f32[256,1,2]{2,1,0:T(1,128)} %stack.2), calls=%async_computation | async-start | bytes 262144 | tf_op jit(solution)/shard_map/all_to_all | solution.py:13
  102.2 12.9 %all-to-all-done = f32[256,1,2]{2,1,0:T(1,128)S(1)} async-done(((f32[256,1,2]{2,1,0:T(1,128)}), f32[256,1,2]{2,1,0:T(1,128)S(1)}, u32[]{:S(2)}, u32[]{:S(2)}) %all-to-all-start) | async-done | bytes 2080 | tf_op jit(solution)/shard_map/all_to_all | solution.py:13
  116.3 0.7 dynamic-slice.1
  117.0 0.6 dynamic-slice
  117.6 1.2 fusion.19
  118.8 1.2 fusion.20
  121.3 0.6 fusion.21
  121.9 5.7 %add_multiply_fusion = f32[1,1024,1024]{1,2,0:T(8,128)} fusion(f32[]{:T(128)} %bitcast.32, f32[1024,8,128]{0,2,1:T(8,128)} %copy-done, f32[1024]{0:T(1024)S(1)} %bitcast.66), kind=kLoop, calls=%fused_computation.5 | loop fusion | flops 3145728 | bytes 8392708 | tf_op jit(solution)/shard_map/div | solution.py:144
  127.6 5.3 %copy.33 = f32[1,1024,1024]{2,1,0:T(8,128)} copy(f32[1,1024,1024]{1,2,0:T(8,128)} %add_multiply_fusion) | data formatting | bytes 8388608 | tf_op jit(solution)/shard_map/div | solution.py:144
  (56 shorter events, 4.6 us)
Async XLA Ops:
  1.0 22.1 %collective-permute-start.1 = (f32[1,1,1024]{1,2,0:T(8,128)S(1)}, f32[1,1,1024]{1,2,0:T(8,128)S(1)}, u32[]{:S(2)}, u32[]{:S(2)}) collective-permute-start(f32[1,1,1024]{1,2,0:T(8,128)S(1)} %copy.28), channel_id=1, source_target_pairs={{0,16},{16,32},{32,48},{48,64},{64,80},{80,96},{96,112},{112,128},... | collective-permute-start | bytes 12296 | tf_op jit(solution)/shard_map/ppermute | solution.py:24
  5.3 16.3 %collective-permute-start.2 = (f32[1,1,1024]{1,2,0:T(8,128)S(1)}, f32[1,1,1024]{1,2,0:T(8,128)S(1)}, u32[]{:S(2)}, u32[]{:S(2)}) collective-permute-start(f32[1,1,1024]{1,2,0:T(8,128)S(1)} %copy.29), channel_id=1, source_target_pairs={{16,0},{32,16},{48,32},{64,48},{80,64},{96,80},{112,96},{128,112},... | collective-permute-start | bytes 12296 | tf_op jit(solution)/shard_map/ppermute | solution.py:25
  12.7 9.2 %collective-permute-start.3 = (f32[1,1024,1]{1,2,0:T(1,128)S(1)}, f32[1,1024,1]{1,2,0:T(1,128)S(1)}, u32[]{:S(2)}, u32[]{:S(2)}) collective-permute-start(f32[1,1024,1]{1,2,0:T(1,128)S(1)} %get-tuple-element.13), channel_id=1, source_target_pairs={{1,0},{2,1},{3,2},{4,3},{5,4},{6,5},{7,6},{8,7},{9,8},{10,9},{11,1... | collective-permute-start | bytes 12296 | tf_op jit(solution)/shard_map/ppermute | solution.py:25
  15.6 14.0 %collective-permute-start = (f32[1,1024,1]{1,2,0:T(1,128)S(1)}, f32[1,1024,1]{1,2,0:T(1,128)S(1)}, u32[]{:S(2)}, u32[]{:S(2)}) collective-permute-start(f32[1,1024,1]{1,2,0:T(1,128)S(1)} %get-tuple-element.14), channel_id=1, source_target_pairs={{0,1},{1,2},{2,3},{3,4},{4,5},{5,6},{6,7},{7,8},{8,9},{9,10},{10,1... | collective-permute-start | bytes 12296 | tf_op jit(solution)/shard_map/ppermute | solution.py:24
  58.7 2.2 %copy-start.1 = (f32[1,1025,1026]{1,2,0:T(8,128)}, f32[1,1025,1026]{1,2,0:T(8,128)S(1)}, u32[]{:S(2)}) copy-start(f32[1,1025,1026]{1,2,0:T(8,128)S(1)} %multiply_subtract_fusion.1) | copy-start | bytes 12619804
  75.4 5.1 %copy-start = (f32[1024,8,128]{0,2,1:T(8,128)}, f32[1024,8,128]{0,2,1:T(8,128)S(1)}, u32[]{:S(2)}) copy-start(f32[1024,8,128]{0,2,1:T(8,128)S(1)} %convolution_add_fusion) | copy-start | bytes 12582916
  86.9 28.2 %all-to-all-start = ((f32[256,1,2]{2,1,0:T(1,128)}), f32[256,1,2]{2,1,0:T(1,128)S(1)}, u32[]{:S(2)}, u32[]{:S(2)}) async-start(f32[256,1,2]{2,1,0:T(1,128)} %stack.2), calls=%async_computation | async-start | bytes 262144 | tf_op jit(solution)/shard_map/all_to_all | solution.py:13
